TPU v7x, 32 devices: a whole 2x2x4 slice. The times are simulated.
32 devices in a mesh: seq: 16 (over z, x, core), head: 2 (over y).
Axes of the slice: x: 2, y: 2, z: 4, core: 2. Of those that a mesh axis runs over, the one named last changes fastest.
Arguments:
- prompt_token_query: bfloat16 [512, 8192], P('seq', 'head'), may hold values from -6 to 6
- prompt_token_key: bfloat16 [512, 1024], P('seq', 'head'), may hold values from -6 to 6
- prompt_token_value: bfloat16 [512, 1024], P('seq', 'head'), may hold values from -6 to 6
- response_query_slots: bfloat16 [3072, 8192], P('seq', 'head'), may hold values from -160 to 160
- response_key_slots: bfloat16 [3072, 1024], P('seq', 'head'), may hold values from -6 to 6
- response_value_slots: bfloat16 [3072, 1024], P('seq', 'head'), may hold values from -6 to 6
- lengths: int32 [4], replicated, may hold values from 1 to 8, 16 in all
- block_table: int32 [16], replicated, may hold values from 0 to 15, each once
Outputs:
- prompt_out: bfloat16 [512, 8192], P(('seq', 'head'))
- answer_out: bfloat16 [3072, 8192], P(('seq', 'head'))
Inputs may be any that keep to these rules, and one draw needn't show every extreme that they name: `lengths`: they sum to 16; the largest is exactly 8. `block_table`: A permutation of 0 to 15.
All inputs are finite; a program needn't handle non-finite values.
Results may differ from a plain program's by a relative error of at most 0.007.
Values may be sent and summed in bfloat16 or wider, within the bound.
A program may use at most 64 MiB of HBM per device.

v0:
```python
import math
import jax
import jax.numpy as jnp
from jax import lax
from jax.sharding import PartitionSpec as P

HEAD_SIZE = 128
RESPONSE_BLOCK = 192
NEG_FILL = -1e30


def block_roles(lengths, global_blocks):
    bounds = jnp.cumsum(lengths)
    member = jnp.sum((global_blocks[:, None] >= bounds[None, :]).astype(jnp.int32), axis=1)
    starts = bounds - lengths
    owner_match = member[:, None] == jnp.arange(lengths.shape[0], dtype=jnp.int32)[None, :]
    first_block = jnp.sum(jnp.where(owner_match, starts[None, :], 0), axis=1)
    return (member, global_blocks - first_block, first_block)


def empty_state(row_count, heads_kv, query_group_width):
    peak_value = jnp.full((row_count, heads_kv, query_group_width), NEG_FILL, jnp.float32)
    weight_total = jnp.zeros((row_count, heads_kv, query_group_width), jnp.float32)
    mixed_sum = jnp.zeros((row_count, heads_kv, query_group_width, HEAD_SIZE), jnp.float32)
    return (peak_value, weight_total, mixed_sum)


def score_block(query_matrix, key_rows):
    return jnp.einsum(
        "rjgd,sjd->rjgs", query_matrix, key_rows, preferred_element_type=jnp.float32
    ) * HEAD_SIZE ** (-0.5)


def absorb(softmax_state, scores, visible, value_rows):
    peak_old, total_old, mixed_old = softmax_state
    masked = jnp.where(visible, scores, NEG_FILL)
    peak_new = jnp.maximum(peak_old, jnp.max(masked, axis=-1))
    factor = jnp.exp(peak_old - peak_new)
    weights = jnp.where(visible, jnp.exp(scores - peak_new[..., None]), 0.0)
    total_new = total_old * factor + jnp.sum(weights, axis=-1)
    mixed_new = mixed_old * factor[..., None] + jnp.einsum(
        "rjgs,sjd->rjgd",
        weights.astype(jnp.bfloat16),
        value_rows,
        preferred_element_type=jnp.float32,
    )
    return (peak_new, total_new, mixed_new)


def finish(softmax_state):
    peak_value, weight_total, mixed_sum = softmax_state
    row_count = mixed_sum.shape[0]
    return (mixed_sum / weight_total[..., None]).astype(jnp.bfloat16).reshape(row_count, -1)


def on_device(
    prompt_token_query,
    prompt_token_key,
    prompt_token_value,
    response_query_slots,
    response_key_slots,
    response_value_slots,
    lengths,
    block_table,
):
    heads_kv = response_key_slots.shape[1] // HEAD_SIZE
    heads_query = response_query_slots.shape[1] // HEAD_SIZE
    query_group_width = heads_query // heads_kv
    shard_rows = response_query_slots.shape[0]
    slot_count = shard_rows // RESPONSE_BLOCK
    prompt_rows = prompt_token_query.shape[0]
    most_blocks = block_table.shape[0] // 2
    batch_blocks = 4
    seq_place = lax.axis_index("seq")
    own_blocks = lax.dynamic_slice_in_dim(block_table, seq_place * slot_count, slot_count, 0)
    own_member, own_position, unused_first = block_roles(lengths, own_blocks)
    answer_queries = response_query_slots.reshape(
        slot_count, RESPONSE_BLOCK, heads_kv, query_group_width, HEAD_SIZE
    )
    prompt_queries = prompt_token_query.reshape(prompt_rows, heads_kv, query_group_width, HEAD_SIZE)
    prompt_positions = seq_place * prompt_rows + jnp.arange(prompt_rows, dtype=jnp.int32)
    initial = (
        tuple(
            (
                empty_state(RESPONSE_BLOCK, heads_kv, query_group_width)
                for slot_ordinal in range(slot_count)
            )
        ),
        empty_state(prompt_rows, heads_kv, query_group_width),
    )
    carried = initial
    piece_key = lax.all_gather(prompt_token_key, "seq", axis=0, tiled=True)
    piece_value = lax.all_gather(prompt_token_value, "seq", axis=0, tiled=True)
    row_count = piece_key.shape[0]
    part_width = math.gcd(row_count, prompt_rows * max(1, 256 // prompt_rows))
    part_count = row_count // part_width
    key_parts = piece_key.reshape(part_count, part_width, heads_kv, HEAD_SIZE)
    value_parts = piece_value.reshape(part_count, part_width, heads_kv, HEAD_SIZE)
    offsets = jnp.arange(part_count, dtype=jnp.int32) * part_width

    def one_part(state_in, part_data):
        key_rows, value_rows, offset = part_data
        answer_states, prompt_state = state_in
        all_seen = jnp.ones((1, 1, 1, part_width), dtype=bool)
        answer_states = tuple(
            (
                absorb(
                    answer_states[slot_ordinal],
                    score_block(answer_queries[slot_ordinal], key_rows),
                    all_seen,
                    value_rows,
                )
                for slot_ordinal in range(slot_count)
            )
        )
        key_positions = offset + jnp.arange(part_width, dtype=jnp.int32)
        seen = (key_positions[None, :] <= prompt_positions[:, None])[:, None, None, :]
        prompt_state = absorb(prompt_state, score_block(prompt_queries, key_rows), seen, value_rows)
        return ((answer_states, prompt_state), None)

    carried, unused_out = lax.scan(one_part, carried, (key_parts, value_parts, offsets))
    finished = carried
    piece_key = lax.all_gather(response_key_slots, "seq", axis=0, tiled=True)
    piece_value = lax.all_gather(response_value_slots, "seq", axis=0, tiled=True)
    block_total = piece_key.shape[0] // RESPONSE_BLOCK
    batch_count = -(-min(most_blocks, block_total) // batch_blocks)
    picked_total = batch_count * batch_blocks
    blocked_keys = piece_key.reshape(block_total, RESPONSE_BLOCK, heads_kv, HEAD_SIZE)
    blocked_values = piece_value.reshape(block_total, RESPONSE_BLOCK, heads_kv, HEAD_SIZE)
    piece_member, piece_position, unused_start = block_roles(lengths, block_table)
    block_ids = jnp.arange(block_total, dtype=jnp.int32)
    answer_states, prompt_state = finished
    slot_ordinal = 0
    wanted = (piece_member == own_member[slot_ordinal]) & (
        piece_position <= own_position[slot_ordinal]
    )
    ranking = jnp.cumsum(wanted.astype(jnp.int32)) - 1
    matches = wanted[None, :] & (
        ranking[None, :] == jnp.arange(picked_total, dtype=jnp.int32)[:, None]
    )
    chosen = jnp.sum(jnp.where(matches, block_ids[None, :], 0), axis=1)
    chosen_live = jnp.any(matches, axis=1)
    chosen_start = piece_position[chosen] * RESPONSE_BLOCK
    query_positions = own_position[slot_ordinal] * RESPONSE_BLOCK + jnp.arange(
        RESPONSE_BLOCK, dtype=jnp.int32
    )
    query_matrix = answer_queries[slot_ordinal]

    def one_batch(state_in, batch_data, query_matrix=query_matrix, query_positions=query_positions):
        picked, live_flags, starts_of = batch_data

        def take_in(state_now):
            key_rows = jnp.take(blocked_keys, picked, axis=0).reshape(
                batch_blocks * RESPONSE_BLOCK, heads_kv, HEAD_SIZE
            )
            value_rows = jnp.take(blocked_values, picked, axis=0).reshape(
                batch_blocks * RESPONSE_BLOCK, heads_kv, HEAD_SIZE
            )
            key_positions = (
                starts_of[:, None] + jnp.arange(RESPONSE_BLOCK, dtype=jnp.int32)[None, :]
            ).reshape(-1)
            key_live = jnp.repeat(live_flags, RESPONSE_BLOCK)
            seen = (key_live[None, :] & (key_positions[None, :] <= query_positions[:, None]))[
                :, None, None, :
            ]
            return absorb(state_now, score_block(query_matrix, key_rows), seen, value_rows)

        def keep_state(state_now):
            return state_now

        return (lax.cond(jnp.any(live_flags), take_in, keep_state, state_in), None)

    batch_inputs = (
        chosen.reshape(batch_count, batch_blocks),
        chosen_live.reshape(batch_count, batch_blocks),
        chosen_start.reshape(batch_count, batch_blocks),
    )
    new_state, unused_out = lax.scan(one_batch, answer_states[slot_ordinal], batch_inputs)
    updated = [new_state]
    finished = (tuple(updated), prompt_state)
    answer_states, prompt_state = finished
    answer_rows = jnp.concatenate([finish(state_item) for state_item in answer_states], axis=0)
    prompt_result = finish(prompt_state)
    prompt_out, answer_out = (
        lax.all_to_all(prompt_result, "head", split_axis=0, concat_axis=1, tiled=True),
        lax.all_to_all(answer_rows, "head", split_axis=0, concat_axis=1, tiled=True),
    )
    return (prompt_out, answer_out)


def solution(mesh):
    in_specs = (
        P("seq", "head"),
        P("seq", "head"),
        P("seq", "head"),
        P("seq", "head"),
        P("seq", "head"),
        P("seq", "head"),
        P(),
        P(),
    )
    out_specs = (P(("seq", "head"), None), P(("seq", "head"), None))
    return jax.shard_map(
        on_device, mesh=mesh, in_specs=in_specs, out_specs=out_specs, check_vma=False
    )
```

profile of v0, /device:TPU:1, one launch (start us, length us, event | category | flops | bytes accessed | tf_op | source)
XLA Modules:
  0.0 202.9 jit_solution(6942071327549159299)
XLA Ops:
  9.8 26.5 %all_gather.12 = bf16[512,512]{1,0:T(8,128)(2,1)} all-gather(bf16[32,512]{1,0:T(8,128)(2,1)} %param.17), channel_id=1, replica_groups=mesh['seq'=16,'head'=2] {'seq'}, dimensions={0}, use_global_device_ids=true | all-gather | bytes 557056 | tf_op jit(solution)/shard_map/all_gather | solution.py:92
  36.4 2.0 reshape.234
  38.4 22.9 %all_gather.13 = bf16[512,512]{1,0:T(8,128)(2,1)} all-gather(bf16[32,512]{1,0:T(8,128)(2,1)} %param.18), channel_id=1, replica_groups=mesh['seq'=16,'head'=2] {'seq'}, dimensions={0}, use_global_device_ids=true | all-gather | bytes 557056 | tf_op jit(solution)/shard_map/all_gather | solution.py:93
  61.2 2.0 reshape.235
  63.2 21.0 %while.37 = (s32[]{:T(128)}, f32[192,4,8]{0,2,1:T(8,128)S(1)}, f32[192,4,8]{0,2,1:T(8,128)S(1)}, f32[192,4,8,128]{3,0,2,1:T(8,128)S(1)}, f32[32,4,8]{0,2,1:T(8,1...) while((s32[]{:T(128)}, f32[192,4,8]{0,2,1:T(8,128)S(1)}, ...), condition=%wide.region_5.6_spmd.clone, body=%wide.region_0.5_spmd.clone.sunk | while | flops 957263104 | bytes 47417864 | solution.py:121
  69.1 2.2 %fusion.63 = f32[192,4,8]{0,2,1:T(8,128)S(1)} fusion(f32[4,256,192,8]{1,2,3,0:T(8,128)S(1)} %get-tuple-element.626, f32[192,4,8]{0,2,1:T(8,128)S(1)} %select_maximum_fusion.4), kind=kLoop, calls=%fused_computation.9.clone.1 | loop fusion | flops 4712448 | bytes 6340608 | tf_op jit(solution)/shard_map/while/body/eval_jaxpr/reduce_sum | solution.py:40
  71.4 2.3 %bitcast_add_fusion.3 = f32[192,4,8,128]{3,0,2,1:T(8,128)S(1)} fusion(f32[192,4,8,128]{3,0,2,1:T(8,128)S(1)} %get-tuple-element.658, f32[4,256,192,8]{1,2,3,0:T(8,128)S(1)} %get-tuple-element.626, f32[192,4,8]{0,2,1:T(8,128)S(1)} %select_maximum_fusion.4, f32[192,4,8]{0,2,1:T(8,128)S(1)} %get-tuple-element.628, pred[]{:T(512)S(6)} %compare.3, ...), kind=kOutput, calls=%fused_computation.11.clone.1 | convolution fusion | flops 409731072 | bytes 12894209 | tf_op jit(solution)/shard_map/while/body/eval_jaxpr/rjgs,sjd->rjgd/dot_general | solution.py:41
  79.6 2.2 %fusion.63 = f32[192,4,8]{0,2,1:T(8,128)S(1)} fusion(f32[4,256,192,8]{1,2,3,0:T(8,128)S(1)} %get-tuple-element.626, f32[192,4,8]{0,2,1:T(8,128)S(1)} %select_maximum_fusion.4), kind=kLoop, calls=%fused_computation.9.clone.1 | loop fusion | flops 4712448 | bytes 6340608 | tf_op jit(solution)/shard_map/while/body/eval_jaxpr/reduce_sum | solution.py:40
  81.9 2.3 %bitcast_add_fusion.3 = f32[192,4,8,128]{3,0,2,1:T(8,128)S(1)} fusion(f32[192,4,8,128]{3,0,2,1:T(8,128)S(1)} %get-tuple-element.658, f32[4,256,192,8]{1,2,3,0:T(8,128)S(1)} %get-tuple-element.626, f32[192,4,8]{0,2,1:T(8,128)S(1)} %select_maximum_fusion.4, f32[192,4,8]{0,2,1:T(8,128)S(1)} %get-tuple-element.628, pred[]{:T(512)S(6)} %compare.3, ...), kind=kOutput, calls=%fused_computation.11.clone.1 | convolution fusion | flops 409731072 | bytes 12894209 | tf_op jit(solution)/shard_map/while/body/eval_jaxpr/rjgs,sjd->rjgd/dot_general | solution.py:41
  86.3 1.8 all_to_all.28
  88.0 4.3 %all-to-all-start = ((bf16[2,16,4096]{2,1,0:T(8,128)(2,1)}), bf16[2,16,4096]{2,1,0:T(8,128)(2,1)}, u32[]{:S(2)}, u32[]{:S(2)}) async-start(bf16[2,16,4096]{2,1,0:T(8,128)(2,1)} %all_to_all.28), calls=%async_computation | async-start | bytes 524288 | tf_op jit(solution)/shard_map/all_to_all | solution.py:185
  99.1 1.8 copy.62
  102.7 5.5 %reshape.241 = bf16[16,192,4,128]{3,2,1,0:T(4,128)(2,1)} reshape(bf16[3072,512]{1,0:T(8,128)(2,1)} %all-gather.3.cloned.1.call-done) | data formatting | bytes 6291456 | tf_op jit(solution)/shard_map/reshape | solution.py:128
  108.2 5.5 %reshape.242 = bf16[16,192,4,128]{3,2,1,0:T(4,128)(2,1)} reshape(bf16[3072,512]{1,0:T(8,128)(2,1)} %all-gather.5.cloned.1.call-done) | data formatting | bytes 6291456 | tf_op jit(solution)/shard_map/reshape | solution.py:129
  113.7 62.2 %while.36 = (s32[]{:T(128)}, f32[192,4,8]{0,2,1:T(8,128)S(1)}, f32[192,4,8]{0,2,1:T(8,128)S(1)}, f32[192,4,8,128]{3,0,2,1:T(8,128)S(1)}, pred[2,4]{1,0:T(4,128)(...) while((s32[]{:T(128)}, f32[192,4,8]{0,2,1:T(8,128)S(1)}, ...), condition=%wide.region_20.22_spmd.clone, body=%wide.region_14.21_spmd.clone.sunk | while | flops 2470492160 | bytes 155146736 | solution.py:178
  115.2 29.7 %conditional.3 = ((f32[192,4,8]{0,2,1:T(8,128)S(1)}, f32[192,4,8]{0,2,1:T(8,128)S(1)}, f32[192,4,8,128]{3,0,2,1:T(8,128)S(1)})) conditional(s32[]{:T(128)} %convert_element_type.62, (f32[192,4,8]{0,2,1:T(8,128)S(1)}, f32[192,4,8]{0,2,1:T(8,128)S(1)}, f32[192,4,8,128]{3,0,2,1:T(8,128)S(1)}) %tuple.83, (pred[1,4]{1,0:T(4,128)(4,1)S(1)}, ...), branch_computations={%region_16.16_spmd, %region_17.20_spmd} | conditional | flops 2470492160 | bytes 155145696 | solution.py:171
  115.5 3.9 %gather_fusion.1 = bf16[4,192,4,128]{3,2,1,0:T(4,128)(2,1)} fusion(bf16[16,192,4,128]{3,2,1,0:T(4,128)(2,1)} %get-tuple-element.205, s32[1024]{0:T(1024)S(1)} %pad_clamp_fusion), kind=kCustom, calls=%fused_computation.1.clone | custom fusion | bytes 1572880 | tf_op jit(solution)/shard_map/while/body/eval_jaxpr/cond/branch_1_fun/jit(_take)/gather | solution.py:156
  119.5 4.0 %gather_fusion = bf16[4,192,4,128]{3,2,1,0:T(4,128)(2,1)} fusion(bf16[16,192,4,128]{3,2,1,0:T(4,128)(2,1)} %get-tuple-element.200, s32[1024]{0:T(1024)S(1)} %pad_clamp_fusion), kind=kCustom, calls=%fused_computation.clone | custom fusion | bytes 1572880 | tf_op jit(solution)/shard_map/while/body/eval_jaxpr/cond/branch_1_fun/jit(_take)/gather | solution.py:153
  123.4 2.2 %broadcast_select_fusion = (bf16[4,192,4,128]{3,2,1,0:T(4,128)(2,1)S(1)}, bf16[4,192,4,128]{3,2,1,0:T(4,128)(2,1)S(1)}) fusion(bf16[4,192,4,128]{3,2,1,0:T(4,128)(2,1)} %gather_fusion.1, pred[4]{0:T(512)(128)(4,1)S(1)} %get-tuple-element.439, bf16[4,192,4,128]{3,2,1,0:T(4,128)(2,1)} %gather_fusion), kind=kLoop, calls=%fused_computation.59 | loop fusion | flops 786432 | bytes 3145732 | tf_op jit(solution)/shard_map/while/body/eval_jaxpr/cond/branch_1_fun/jit(_take)/select_n | solution.py:156
  125.8 3.5 %fusion.27 = (f32[192,4,8]{0,2,1:T(8,128)S(1)}, f32[4,768,192,8]{1,2,3,0:T(8,128)S(1)}) fusion(pred[192,768]{1,0:T(8,128)(4,1)S(1)} %compare_and_fusion, bf16[192,4,8,128]{3,0,2,1:T(8,128)(2,1)S(1)} %copy-done.2, bf16[768,4,128,1]{2,1,0,3:T(4,128)(2,1)S(1)} %bitcast.130), kind=kOutput, calls=%fused_computation.48 | convolution fusion | flops 1222109184 | bytes 21405696 | tf_op jit(solution)/shard_map/while/body/eval_jaxpr/cond/branch_1_fun/rjgd,sjd->rjgs/dot_general | solution.py:29
  129.4 5.4 %fusion.31 = f32[192,4,8]{0,2,1:T(8,128)S(1)} fusion(f32[4,768,192,8]{1,2,3,0:T(8,128)S(1)} %get-tuple-element.457, f32[192,4,8]{0,2,1:T(8,128)S(1)} %max.10, pred[192,768]{1,0:T(8,128)(4,1)S(1)} %compare_and_fusion), kind=kLoop, calls=%fused_computation.52 | loop fusion | flops 18868224 | bytes 19070976 | tf_op jit(solution)/shard_map/while/body/eval_jaxpr/cond/branch_1_fun/reduce_sum | solution.py:40
  135.9 9.0 %bitcast_add_fusion.1 = f32[192,4,8,128]{3,0,2,1:T(8,128)S(1)} fusion(f32[192,4,8,128]{3,0,2,1:T(8,128)S(1)} %get-tuple-element.204, f32[4,768,192,8]{1,2,3,0:T(8,128)} %copy-done, f32[192,4,8]{0,2,1:T(8,128)S(1)} %max.10, pred[192,768]{1,0:T(8,128)(4,1)S(1)} %compare_and_fusion, f32[192,4,8]{0,2,1:T(8,128)S(1)} %get-tuple-element.438, ...), kind=kOutput, calls=%fused_computation.55 | convolution fusion | flops 1228406784 | bytes 26148864 | tf_op jit(solution)/shard_map/while/body/eval_jaxpr/cond/branch_1_fun/rjgs,sjd->rjgd/dot_general | solution.py:41
  146.3 29.7 %conditional.3 = ((f32[192,4,8]{0,2,1:T(8,128)S(1)}, f32[192,4,8]{0,2,1:T(8,128)S(1)}, f32[192,4,8,128]{3,0,2,1:T(8,128)S(1)})) conditional(s32[]{:T(128)} %convert_element_type.62, (f32[192,4,8]{0,2,1:T(8,128)S(1)}, f32[192,4,8]{0,2,1:T(8,128)S(1)}, f32[192,4,8,128]{3,0,2,1:T(8,128)S(1)}) %tuple.83, (pred[1,4]{1,0:T(4,128)(4,1)S(1)}, ...), branch_computations={%region_16.16_spmd, %region_17.20_spmd} | conditional | flops 2470492160 | bytes 155145696 | solution.py:171
  146.7 3.9 %gather_fusion.1 = bf16[4,192,4,128]{3,2,1,0:T(4,128)(2,1)} fusion(bf16[16,192,4,128]{3,2,1,0:T(4,128)(2,1)} %get-tuple-element.205, s32[1024]{0:T(1024)S(1)} %pad_clamp_fusion), kind=kCustom, calls=%fused_computation.1.clone | custom fusion | bytes 1572880 | tf_op jit(solution)/shard_map/while/body/eval_jaxpr/cond/branch_1_fun/jit(_take)/gather | solution.py:156
  150.6 4.0 %gather_fusion = bf16[4,192,4,128]{3,2,1,0:T(4,128)(2,1)} fusion(bf16[16,192,4,128]{3,2,1,0:T(4,128)(2,1)} %get-tuple-element.200, s32[1024]{0:T(1024)S(1)} %pad_clamp_fusion), kind=kCustom, calls=%fused_computation.clone | custom fusion | bytes 1572880 | tf_op jit(solution)/shard_map/while/body/eval_jaxpr/cond/branch_1_fun/jit(_take)/gather | solution.py:153
  154.6 2.2 %broadcast_select_fusion = (bf16[4,192,4,128]{3,2,1,0:T(4,128)(2,1)S(1)}, bf16[4,192,4,128]{3,2,1,0:T(4,128)(2,1)S(1)}) fusion(bf16[4,192,4,128]{3,2,1,0:T(4,128)(2,1)} %gather_fusion.1, pred[4]{0:T(512)(128)(4,1)S(1)} %get-tuple-element.439, bf16[4,192,4,128]{3,2,1,0:T(4,128)(2,1)} %gather_fusion), kind=kLoop, calls=%fused_computation.59 | loop fusion | flops 786432 | bytes 3145732 | tf_op jit(solution)/shard_map/while/body/eval_jaxpr/cond/branch_1_fun/jit(_take)/select_n | solution.py:156
  157.0 3.5 %fusion.27 = (f32[192,4,8]{0,2,1:T(8,128)S(1)}, f32[4,768,192,8]{1,2,3,0:T(8,128)S(1)}) fusion(pred[192,768]{1,0:T(8,128)(4,1)S(1)} %compare_and_fusion, bf16[192,4,8,128]{3,0,2,1:T(8,128)(2,1)S(1)} %copy-done.2, bf16[768,4,128,1]{2,1,0,3:T(4,128)(2,1)S(1)} %bitcast.130), kind=kOutput, calls=%fused_computation.48 | convolution fusion | flops 1222109184 | bytes 21405696 | tf_op jit(solution)/shard_map/while/body/eval_jaxpr/cond/branch_1_fun/rjgd,sjd->rjgs/dot_general | solution.py:29
  160.5 5.4 %fusion.31 = f32[192,4,8]{0,2,1:T(8,128)S(1)} fusion(f32[4,768,192,8]{1,2,3,0:T(8,128)S(1)} %get-tuple-element.457, f32[192,4,8]{0,2,1:T(8,128)S(1)} %max.10, pred[192,768]{1,0:T(8,128)(4,1)S(1)} %compare_and_fusion), kind=kLoop, calls=%fused_computation.52 | loop fusion | flops 18868224 | bytes 19070976 | tf_op jit(solution)/shard_map/while/body/eval_jaxpr/cond/branch_1_fun/reduce_sum | solution.py:40
  167.0 9.0 %bitcast_add_fusion.1 = f32[192,4,8,128]{3,0,2,1:T(8,128)S(1)} fusion(f32[192,4,8,128]{3,0,2,1:T(8,128)S(1)} %get-tuple-element.204, f32[4,768,192,8]{1,2,3,0:T(8,128)} %copy-done, f32[192,4,8]{0,2,1:T(8,128)S(1)} %max.10, pred[192,768]{1,0:T(8,128)(4,1)S(1)} %compare_and_fusion, f32[192,4,8]{0,2,1:T(8,128)S(1)} %get-tuple-element.438, ...), kind=kOutput, calls=%fused_computation.55 | convolution fusion | flops 1228406784 | bytes 26148864 | tf_op jit(solution)/shard_map/while/body/eval_jaxpr/cond/branch_1_fun/rjgs,sjd->rjgd/dot_general | solution.py:41
  178.0 2.1 %all_to_all.32 = bf16[2,96,4096]{2,1,0:T(8,128)(2,1)} reshape(bf16[192,4,8,128]{3,2,1,0:T(8,128)(2,1)S(1)} %copy.46) | data formatting | bytes 3145728 | tf_op jit(solution)/shard_map/all_to_all | solution.py:186
  180.1 3.7 %all-to-all-start.1 = ((bf16[2,96,4096]{2,1,0:T(8,128)(2,1)}), bf16[2,96,4096]{2,1,0:T(8,128)(2,1)S(1)}, u32[]{:S(2)}, u32[]{:S(2)}) async-start(bf16[2,96,4096]{2,1,0:T(8,128)(2,1)} %all_to_all.32), calls=%async_computation.1 | async-start | bytes 3145728 | tf_op jit(solution)/shard_map/all_to_all | solution.py:186
  185.4 9.4 %all-to-all-done.1 = bf16[2,96,4096]{2,1,0:T(8,128)(2,1)S(1)} async-done(((bf16[2,96,4096]{2,1,0:T(8,128)(2,1)}), bf16[2,96,4096]{2,1,0:T(8,128)(2,1)S(1)}, u32[]{:S(2)}, u32[]{:S(2)}) %all-to-all-start.1) | async-done | bytes 1572896 | tf_op jit(solution)/shard_map/all_to_all | solution.py:186
  (126 shorter events, 33.3 us)
Async XLA Ops:
  7.2 95.5 %all-gather.3.cloned.1.call-start = ((), (), s32[]{:S(2)}) async-start(), calls=%async_computation.2 | async-start | bytes 3342336 | tf_op jit(solution)/shard_map/all_gather | solution.py:123
  7.9 100.3 %all-gather.5.cloned.1.call-start = ((), (), s32[]{:S(2)}) async-start(), calls=%async_computation.3 | async-start | bytes 3342336 | tf_op jit(solution)/shard_map/all_gather | solution.py:124
  63.2 29.1 %copy-start.5 = (s32[4]{0:T(128)S(1)}, s32[4]{0:T(128)}, u32[]{:S(2)}) copy-start(s32[4]{0:T(128)} %param.22) | copy-start | bytes 52
  63.2 29.3 %copy-start.6 = (s32[16]{0:T(128)S(1)}, s32[16]{0:T(128)}, u32[]{:S(2)}) copy-start(s32[16]{0:T(128)} %param.23) | copy-start | bytes 196
  63.2 3.4 %copy-start.3 = (f32[32,4,8,128]{3,0,2,1:T(8,128)S(1)}, f32[32,4,8,128]{3,0,2,1:T(8,128)}, u32[]{:S(2)}) copy-start(f32[32,4,8,128]{3,0,2,1:T(8,128)} %get-tuple-element.661) | copy-start | bytes 1572868 | tf_op jit(solution)/shard_map/while
  64.5 2.7 %copy-start.1 = (bf16[192,4096]{1,0:T(8,128)(2,1)S(1)}, bf16[192,4096]{1,0:T(8,128)(2,1)}, u32[]{:S(2)}) copy-start(bf16[192,4096]{1,0:T(8,128)(2,1)} %get-tuple-element.678) | copy-start | bytes 4718596 | tf_op jit(solution)/shard_map/while
  67.1 2.0 copy-start.4
  73.7 3.4 %copy-start.3 = (f32[32,4,8,128]{3,0,2,1:T(8,128)S(1)}, f32[32,4,8,128]{3,0,2,1:T(8,128)}, u32[]{:S(2)}) copy-start(f32[32,4,8,128]{3,0,2,1:T(8,128)} %get-tuple-element.661) | copy-start | bytes 1572868 | tf_op jit(solution)/shard_map/while
  75.0 2.7 %copy-start.1 = (bf16[192,4096]{1,0:T(8,128)(2,1)S(1)}, bf16[192,4096]{1,0:T(8,128)(2,1)}, u32[]{:S(2)}) copy-start(bf16[192,4096]{1,0:T(8,128)(2,1)} %get-tuple-element.678) | copy-start | bytes 4718596 | tf_op jit(solution)/shard_map/while
  77.6 2.0 copy-start.4
  88.0 92.1 %all-to-all-start = ((bf16[2,16,4096]{2,1,0:T(8,128)(2,1)}), bf16[2,16,4096]{2,1,0:T(8,128)(2,1)}, u32[]{:S(2)}, u32[]{:S(2)}) async-start(bf16[2,16,4096]{2,1,0:T(8,128)(2,1)} %all_to_all.28), calls=%async_computation | async-start | bytes 524288 | tf_op jit(solution)/shard_map/all_to_all | solution.py:185
  123.4 2.4 %copy-start.2 = (bf16[192,4,8,128]{3,0,2,1:T(8,128)(2,1)S(1)}, bf16[192,4,8,128]{3,0,2,1:T(8,128)(2,1)}, u32[]{:S(2)}) copy-start(bf16[192,4,8,128]{3,0,2,1:T(8,128)(2,1)} %get-tuple-element.202) | copy-start | bytes 4718596 | tf_op jit(solution)/shard_map/while/body/eval_jaxpr/cond
  129.4 6.5 %copy-start = (f32[4,768,192,8]{1,2,3,0:T(8,128)}, f32[4,768,192,8]{1,2,3,0:T(8,128)S(1)}, u32[]{:S(2)}) copy-start(f32[4,768,192,8]{1,2,3,0:T(8,128)S(1)} %get-tuple-element.457) | copy-start | bytes 56623108 | tf_op jit(solution)/shard_map/while/body/eval_jaxpr/cond
  154.6 2.4 %copy-start.2 = (bf16[192,4,8,128]{3,0,2,1:T(8,128)(2,1)S(1)}, bf16[192,4,8,128]{3,0,2,1:T(8,128)(2,1)}, u32[]{:S(2)}) copy-start(bf16[192,4,8,128]{3,0,2,1:T(8,128)(2,1)} %get-tuple-element.202) | copy-start | bytes 4718596 | tf_op jit(solution)/shard_map/while/body/eval_jaxpr/cond
  160.5 6.5 %copy-start = (f32[4,768,192,8]{1,2,3,0:T(8,128)}, f32[4,768,192,8]{1,2,3,0:T(8,128)S(1)}, u32[]{:S(2)}) copy-start(f32[4,768,192,8]{1,2,3,0:T(8,128)S(1)} %get-tuple-element.457) | copy-start | bytes 56623108 | tf_op jit(solution)/shard_map/while/body/eval_jaxpr/cond
  180.1 14.7 %all-to-all-start.1 = ((bf16[2,96,4096]{2,1,0:T(8,128)(2,1)}), bf16[2,96,4096]{2,1,0:T(8,128)(2,1)S(1)}, u32[]{:S(2)}, u32[]{:S(2)}) async-start(bf16[2,96,4096]{2,1,0:T(8,128)(2,1)} %all_to_all.32), calls=%async_computation.1 | async-start | bytes 3145728 | tf_op jit(solution)/shard_map/all_to_all | solution.py:186
Sparse Core Ops, SparseCore 0:
  10.3 50.5 all-gather.2
  63.2 44.9 all-gather.4
where the time goes:
time: 204 us; the launch traced here: 203 us
  local copies, waits for them, and re-layouts  52.9 us (26%)
  blocking collectives  49.4 us (24%)
  matrix products  34.5 us (17%)
  other arithmetic  30.1 us (15%)
  between operations  15.4 us (8%)
  waiting for transfers between devices  10.7 us (5%)
  starting transfers between devices  8.04 us (4%)
    all_gather x1, blocking collectives, on_device(): piece_key = lax.all_gather(prompt_token_key, 'seq', axis=0, tiled=True)  26.5 us
    dot_general x6, matrix products, absorb(): jnp.einsum('rjgs,sjd->rjgd', weights.astype(jnp.bfloat16), value_rows, pr...  23.4 us
    all_gather x1, blocking collectives, on_device(): piece_value = lax.all_gather(prompt_token_value, 'seq', axis=0, tiled=True)  22.9 us
    reduce_sum x6, other arithmetic, absorb(): total_new = total_old * factor + jnp.sum(weights, axis=-1)  15.9 us
    dot_general x6, matrix products, score_block(): jnp.einsum('rjgd,sjd->rjgs', query_matrix, key_rows, preferred_element_ty...  11 us
    all_to_all x1, waiting for transfers between devices, on_device(): lax.all_to_all(answer_rows, 'head', split_axis=0, concat_axis=1, tiled=True)  9.36 us
    gather x2, local copies, waits for them, and re-layouts, take_in(): jnp.take(blocked_keys, picked, axis=0)  7.93 us
    gather x2, local copies, waits for them, and re-layouts, take_in(): jnp.take(blocked_values, picked, axis=0)  7.87 us
  transfers between devices with their start and end apart: 4, of which 1 were waited for; matrix products, arithmetic and copies ran while one was open for 54% of the time, Pallas kernels for 0%

commit v1 on v0

--- a/solution.py
+++ b/solution.py
@@ -89,8 +89,13 @@
         empty_state(prompt_rows, heads_kv, query_group_width),
     )
     carried = initial
-    piece_key = lax.all_gather(prompt_token_key, "seq", axis=0, tiled=True)
-    piece_value = lax.all_gather(prompt_token_value, "seq", axis=0, tiled=True)
+    piece_key, piece_value = jnp.split(
+        lax.all_gather(
+            jnp.concatenate([prompt_token_key, prompt_token_value], 1), "seq", axis=0, tiled=True
+        ),
+        [prompt_token_key.shape[1]],
+        1,
+    )
     row_count = piece_key.shape[0]
     part_width = math.gcd(row_count, prompt_rows * max(1, 256 // prompt_rows))
     part_count = row_count // part_width

time: 204 us -> 240 us (1.18)
  waiting for transfers between devices: 10.7 us -> 88.8 us
  blocking collectives: 49.4 us -> 0 us
  other arithmetic: 30.1 us -> 34.4 us
  local copies, waits for them, and re-layouts: 52.9 us -> 55.8 us
    all_gather x2 -> x0, blocking collectives: 49.4 us -> none  [the longest x1 26.5 us: on_device(): piece_key = lax.all_gather(prompt_token_key, 'seq', axis=0, tiled=True)]
    all_gather x1, waiting for transfers between devices: 0.01 us -> 40.7 us  [on_device(): lax.all_gather(response_value_slots, 'seq', axis=0, tiled=True)]
    all_gather x0 -> x1, waiting for transfers between devices: none -> 26.1 us  [on_device(): lax.all_gather(jnp.concatenate([prompt_token_key, prompt_token_value], 1)...]
    all_gather x1, waiting for transfers between devices: 0.01 us -> 11.2 us  [on_device(): piece_key = lax.all_gather(response_key_slots, 'seq', axis=0, tiled=True)]
  transfers between devices with their start and end apart: 4 -> 5, of which waited for: 1 -> 4; matrix products, arithmetic and copies ran while one was open for 54% -> 49% of each run, Pallas kernels for 0% -> 0%
where the time goes in v1:
time: 240 us; the launch traced here: 238 us
  waiting for transfers between devices  88.8 us (37%)
  local copies, waits for them, and re-layouts  55.8 us (23%)
  matrix products  34.5 us (14%)
  other arithmetic  34.4 us (14%)
  between operations  15.1 us (6%)
  starting transfers between devices  8.08 us (3%)
    all_gather x1, waiting for transfers between devices, on_device(): lax.all_gather(response_value_slots, 'seq', axis=0, tiled=True)  40.7 us
    all_gather x1, waiting for transfers between devices, on_device(): lax.all_gather(jnp.concatenate([prompt_token_key, prompt_token_value], 1)...  26.1 us
    dot_general x6, matrix products, absorb(): jnp.einsum('rjgs,sjd->rjgd', weights.astype(jnp.bfloat16), value_rows, pr...  23.4 us
    reduce_sum x6, other arithmetic, absorb(): total_new = total_old * factor + jnp.sum(weights, axis=-1)  15.9 us
    all_gather x1, waiting for transfers between devices, on_device(): piece_key = lax.all_gather(response_key_slots, 'seq', axis=0, tiled=True)  11.2 us
    dot_general x6, matrix products, score_block(): jnp.einsum('rjgd,sjd->rjgs', query_matrix, key_rows, preferred_element_ty...  11 us
    all_to_all x1, waiting for transfers between devices, on_device(): lax.all_to_all(answer_rows, 'head', split_axis=0, concat_axis=1, tiled=True)  9.36 us
    gather x2, local copies, waits for them, and re-layouts, take_in(): jnp.take(blocked_keys, picked, axis=0)  7.93 us
  transfers between devices with their start and end apart: 5, of which 4 were waited for; matrix products, arithmetic and copies ran while one was open for 49% of the time, Pallas kernels for 0%

profile of v1, /device:TPU:1, one launch (start us, length us, event | category | flops | bytes accessed | tf_op | source)
XLA Modules:
  0.0 238.4 jit_solution(11931580740484169831)
XLA Ops:
  14.3 2.0 fusion.45
  25.0 26.1 %all-gather.4.cloned.1.call-done = bf16[512,1024]{1,0:T(8,128)(2,1)} async-done(((bf16[32,1024]{1,0:T(8,128)(2,1)}), bf16[512,1024]{1,0:T(8,128)(2,1)}) %all-gather.4.cloned.1.call-update) | async-done | bytes 1048592 | tf_op jit(solution)/shard_map/all_gather | solution.py:93
  51.1 2.3 fusion.48
  55.4 2.0 reshape.234
  57.4 21.1 %while.37 = (s32[]{:T(128)}, f32[192,4,8]{0,2,1:T(8,128)S(1)}, f32[192,4,8]{0,2,1:T(8,128)S(1)}, f32[192,4,8,128]{3,0,2,1:T(8,128)S(1)}, f32[32,4,8]{0,2,1:T(8,1...) while((s32[]{:T(128)}, f32[192,4,8]{0,2,1:T(8,128)S(1)}, ...), condition=%wide.region_5.6_spmd.clone, body=%wide.region_0.5_spmd.clone.sunk | while | flops 957263104 | bytes 47417864 | solution.py:126
  63.4 2.2 fusion.64
  65.6 2.3 bitcast_add_fusion.3
  74.0 2.2 fusion.64
  76.2 2.3 bitcast_add_fusion.3
  82.4 4.3 %all-to-all-start = ((bf16[2,16,4096]{2,1,0:T(8,128)(2,1)}), bf16[2,16,4096]{2,1,0:T(8,128)(2,1)}, u32[]{:S(2)}, u32[]{:S(2)}) async-start(bf16[2,16,4096]{2,1,0:T(8,128)(2,1)} %all_to_all.28), calls=%async_computation | async-start | bytes 524288 | tf_op jit(solution)/shard_map/all_to_all | solution.py:190
  86.7 11.2 %all-gather.6.cloned.1.call-done = bf16[3072,512]{1,0:T(8,128)(2,1)} async-done(((bf16[192,512]{1,0:T(8,128)(2,1)}), bf16[3072,512]{1,0:T(8,128)(2,1)}) %all-gather.6.cloned.1.call-update) | async-done | bytes 3145744 | tf_op jit(solution)/shard_map/all_gather | solution.py:128
  97.8 5.5 %reshape.241 = bf16[16,192,4,128]{3,2,1,0:T(4,128)(2,1)} reshape(bf16[3072,512]{1,0:T(8,128)(2,1)} %all-gather.6.cloned.1.call-done) | data formatting | bytes 6291456 | tf_op jit(solution)/shard_map/reshape | solution.py:133
  103.3 40.7 %all-gather.8.cloned.1.call-done = bf16[3072,512]{1,0:T(8,128)(2,1)} async-done(((bf16[192,512]{1,0:T(8,128)(2,1)}), bf16[3072,512]{1,0:T(8,128)(2,1)}) %all-gather.8.cloned.1.call-update) | async-done | bytes 3145744 | tf_op jit(solution)/shard_map/all_gather | solution.py:129
  144.0 5.5 %reshape.242 = bf16[16,192,4,128]{3,2,1,0:T(4,128)(2,1)} reshape(bf16[3072,512]{1,0:T(8,128)(2,1)} %all-gather.8.cloned.1.call-done) | data formatting | bytes 6291456 | tf_op jit(solution)/shard_map/reshape | solution.py:134
  149.5 62.2 %while.36 = (s32[]{:T(128)}, f32[192,4,8]{0,2,1:T(8,128)S(1)}, f32[192,4,8]{0,2,1:T(8,128)S(1)}, f32[192,4,8,128]{3,0,2,1:T(8,128)S(1)}, pred[2,4]{1,0:T(4,128)(...) while((s32[]{:T(128)}, f32[192,4,8]{0,2,1:T(8,128)S(1)}, ...), condition=%wide.region_20.22_spmd.clone, body=%wide.region_14.21_spmd.clone.sunk | while | flops 2470492160 | bytes 155146736 | solution.py:183
  151.0 29.7 %conditional.3 = ((f32[192,4,8]{0,2,1:T(8,128)S(1)}, f32[192,4,8]{0,2,1:T(8,128)S(1)}, f32[192,4,8,128]{3,0,2,1:T(8,128)S(1)})) conditional(s32[]{:T(128)} %convert_element_type.62, (f32[192,4,8]{0,2,1:T(8,128)S(1)}, f32[192,4,8]{0,2,1:T(8,128)S(1)}, f32[192,4,8,128]{3,0,2,1:T(8,128)S(1)}) %tuple.84, (pred[1,4]{1,0:T(4,128)(4,1)S(1)}, ...), branch_computations={%region_16.16_spmd, %region_17.20_spmd} | conditional | flops 2470492160 | bytes 155145696 | solution.py:176
  151.3 3.9 %gather_fusion.1 = bf16[4,192,4,128]{3,2,1,0:T(4,128)(2,1)} fusion(bf16[16,192,4,128]{3,2,1,0:T(4,128)(2,1)} %get-tuple-element.205, s32[1024]{0:T(1024)S(1)} %pad_clamp_fusion), kind=kCustom, calls=%fused_computation.1.clone | custom fusion | bytes 1572880 | tf_op jit(solution)/shard_map/while/body/eval_jaxpr/cond/branch_1_fun/jit(_take)/gather | solution.py:161
  155.3 4.0 %gather_fusion = bf16[4,192,4,128]{3,2,1,0:T(4,128)(2,1)} fusion(bf16[16,192,4,128]{3,2,1,0:T(4,128)(2,1)} %get-tuple-element.200, s32[1024]{0:T(1024)S(1)} %pad_clamp_fusion), kind=kCustom, calls=%fused_computation.clone | custom fusion | bytes 1572880 | tf_op jit(solution)/shard_map/while/body/eval_jaxpr/cond/branch_1_fun/jit(_take)/gather | solution.py:158
  159.2 2.2 broadcast_select_fusion
  161.6 3.5 %fusion.27 = (f32[192,4,8]{0,2,1:T(8,128)S(1)}, f32[4,768,192,8]{1,2,3,0:T(8,128)S(1)}) fusion(pred[192,768]{1,0:T(8,128)(4,1)S(1)} %compare_and_fusion, bf16[192,4,8,128]{3,0,2,1:T(8,128)(2,1)S(1)} %copy-done.2, bf16[768,4,128,1]{2,1,0,3:T(4,128)(2,1)S(1)} %bitcast.130), kind=kOutput, calls=%fused_computation.48 | convolution fusion | flops 1222109184 | bytes 21405696 | tf_op jit(solution)/shard_map/while/body/eval_jaxpr/cond/branch_1_fun/rjgd,sjd->rjgs/dot_general | solution.py:29
  165.2 5.4 %fusion.31 = f32[192,4,8]{0,2,1:T(8,128)S(1)} fusion(f32[4,768,192,8]{1,2,3,0:T(8,128)S(1)} %get-tuple-element.457, f32[192,4,8]{0,2,1:T(8,128)S(1)} %max.10, pred[192,768]{1,0:T(8,128)(4,1)S(1)} %compare_and_fusion), kind=kLoop, calls=%fused_computation.52 | loop fusion | flops 18868224 | bytes 19070976 | tf_op jit(solution)/shard_map/while/body/eval_jaxpr/cond/branch_1_fun/reduce_sum | solution.py:40
  171.7 9.0 %bitcast_add_fusion.1 = f32[192,4,8,128]{3,0,2,1:T(8,128)S(1)} fusion(f32[192,4,8,128]{3,0,2,1:T(8,128)S(1)} %get-tuple-element.204, f32[4,768,192,8]{1,2,3,0:T(8,128)} %copy-done, f32[192,4,8]{0,2,1:T(8,128)S(1)} %max.10, pred[192,768]{1,0:T(8,128)(4,1)S(1)} %compare_and_fusion, f32[192,4,8]{0,2,1:T(8,128)S(1)} %get-tuple-element.438, ...), kind=kOutput, calls=%fused_computation.55 | convolution fusion | flops 1228406784 | bytes 26148864 | tf_op jit(solution)/shard_map/while/body/eval_jaxpr/cond/branch_1_fun/rjgs,sjd->rjgd/dot_general | solution.py:41
  182.1 29.7 %conditional.3 = ((f32[192,4,8]{0,2,1:T(8,128)S(1)}, f32[192,4,8]{0,2,1:T(8,128)S(1)}, f32[192,4,8,128]{3,0,2,1:T(8,128)S(1)})) conditional(s32[]{:T(128)} %convert_element_type.62, (f32[192,4,8]{0,2,1:T(8,128)S(1)}, f32[192,4,8]{0,2,1:T(8,128)S(1)}, f32[192,4,8,128]{3,0,2,1:T(8,128)S(1)}) %tuple.84, (pred[1,4]{1,0:T(4,128)(4,1)S(1)}, ...), branch_computations={%region_16.16_spmd, %region_17.20_spmd} | conditional | flops 2470492160 | bytes 155145696 | solution.py:176
  182.5 3.9 %gather_fusion.1 = bf16[4,192,4,128]{3,2,1,0:T(4,128)(2,1)} fusion(bf16[16,192,4,128]{3,2,1,0:T(4,128)(2,1)} %get-tuple-element.205, s32[1024]{0:T(1024)S(1)} %pad_clamp_fusion), kind=kCustom, calls=%fused_computation.1.clone | custom fusion | bytes 1572880 | tf_op jit(solution)/shard_map/while/body/eval_jaxpr/cond/branch_1_fun/jit(_take)/gather | solution.py:161
  186.4 4.0 %gather_fusion = bf16[4,192,4,128]{3,2,1,0:T(4,128)(2,1)} fusion(bf16[16,192,4,128]{3,2,1,0:T(4,128)(2,1)} %get-tuple-element.200, s32[1024]{0:T(1024)S(1)} %pad_clamp_fusion), kind=kCustom, calls=%fused_computation.clone | custom fusion | bytes 1572880 | tf_op jit(solution)/shard_map/while/body/eval_jaxpr/cond/branch_1_fun/jit(_take)/gather | solution.py:158
  190.4 2.2 broadcast_select_fusion
  192.8 3.5 %fusion.27 = (f32[192,4,8]{0,2,1:T(8,128)S(1)}, f32[4,768,192,8]{1,2,3,0:T(8,128)S(1)}) fusion(pred[192,768]{1,0:T(8,128)(4,1)S(1)} %compare_and_fusion, bf16[192,4,8,128]{3,0,2,1:T(8,128)(2,1)S(1)} %copy-done.2, bf16[768,4,128,1]{2,1,0,3:T(4,128)(2,1)S(1)} %bitcast.130), kind=kOutput, calls=%fused_computation.48 | convolution fusion | flops 1222109184 | bytes 21405696 | tf_op jit(solution)/shard_map/while/body/eval_jaxpr/cond/branch_1_fun/rjgd,sjd->rjgs/dot_general | solution.py:29
  196.3 5.4 %fusion.31 = f32[192,4,8]{0,2,1:T(8,128)S(1)} fusion(f32[4,768,192,8]{1,2,3,0:T(8,128)S(1)} %get-tuple-element.457, f32[192,4,8]{0,2,1:T(8,128)S(1)} %max.10, pred[192,768]{1,0:T(8,128)(4,1)S(1)} %compare_and_fusion), kind=kLoop, calls=%fused_computation.52 | loop fusion | flops 18868224 | bytes 19070976 | tf_op jit(solution)/shard_map/while/body/eval_jaxpr/cond/branch_1_fun/reduce_sum | solution.py:40
  202.8 9.0 %bitcast_add_fusion.1 = f32[192,4,8,128]{3,0,2,1:T(8,128)S(1)} fusion(f32[192,4,8,128]{3,0,2,1:T(8,128)S(1)} %get-tuple-element.204, f32[4,768,192,8]{1,2,3,0:T(8,128)} %copy-done, f32[192,4,8]{0,2,1:T(8,128)S(1)} %max.10, pred[192,768]{1,0:T(8,128)(4,1)S(1)} %compare_and_fusion, f32[192,4,8]{0,2,1:T(8,128)S(1)} %get-tuple-element.438, ...), kind=kOutput, calls=%fused_computation.55 | convolution fusion | flops 1228406784 | bytes 26148864 | tf_op jit(solution)/shard_map/while/body/eval_jaxpr/cond/branch_1_fun/rjgs,sjd->rjgd/dot_general | solution.py:41
  213.8 2.1 all_to_all.32
  215.9 3.7 %all-to-all-start.1 = ((bf16[2,96,4096]{2,1,0:T(8,128)(2,1)}), bf16[2,96,4096]{2,1,0:T(8,128)(2,1)S(1)}, u32[]{:S(2)}, u32[]{:S(2)}) async-start(bf16[2,96,4096]{2,1,0:T(8,128)(2,1)} %all_to_all.32), calls=%async_computation.1 | async-start | bytes 3145728 | tf_op jit(solution)/shard_map/all_to_all | solution.py:191
  221.2 9.4 %all-to-all-done.1 = bf16[2,96,4096]{2,1,0:T(8,128)(2,1)S(1)} async-done(((bf16[2,96,4096]{2,1,0:T(8,128)(2,1)}), bf16[2,96,4096]{2,1,0:T(8,128)(2,1)S(1)}, u32[]{:S(2)}, u32[]{:S(2)}) %all-to-all-start.1) | async-done | bytes 1572896 | tf_op jit(solution)/shard_map/all_to_all | solution.py:191
  (125 shorter events, 41.8 us)
Async XLA Ops:
  7.2 44.0 %all-gather.4.cloned.1.call-start = ((), (), s32[]{:S(2)}) async-start(), calls=%async_computation.2 | async-start | bytes 1114112 | tf_op jit(solution)/shard_map/all_gather | solution.py:93
  8.6 89.2 %all-gather.6.cloned.1.call-start = ((), (), s32[]{:S(2)}) async-start(), calls=%async_computation.3 | async-start | bytes 3342336 | tf_op jit(solution)/shard_map/all_gather | solution.py:128
  9.4 134.6 %all-gather.8.cloned.1.call-start = ((), (), s32[]{:S(2)}) async-start(), calls=%async_computation.4 | async-start | bytes 3342336 | tf_op jit(solution)/shard_map/all_gather | solution.py:129
  57.4 3.5 %copy-start.3 = (f32[32,4,8,128]{3,0,2,1:T(8,128)S(1)}, f32[32,4,8,128]{3,0,2,1:T(8,128)}, u32[]{:S(2)}) copy-start(f32[32,4,8,128]{3,0,2,1:T(8,128)} %get-tuple-element.663) | copy-start | bytes 1572868 | tf_op jit(solution)/shard_map/while
  58.7 2.7 %copy-start.1 = (bf16[192,4096]{1,0:T(8,128)(2,1)S(1)}, bf16[192,4096]{1,0:T(8,128)(2,1)}, u32[]{:S(2)}) copy-start(bf16[192,4096]{1,0:T(8,128)(2,1)} %get-tuple-element.680) | copy-start | bytes 4718596 | tf_op jit(solution)/shard_map/while
  61.4 2.0 copy-start.4
  68.0 3.5 %copy-start.3 = (f32[32,4,8,128]{3,0,2,1:T(8,128)S(1)}, f32[32,4,8,128]{3,0,2,1:T(8,128)}, u32[]{:S(2)}) copy-start(f32[32,4,8,128]{3,0,2,1:T(8,128)} %get-tuple-element.663) | copy-start | bytes 1572868 | tf_op jit(solution)/shard_map/while
  69.3 2.7 %copy-start.1 = (bf16[192,4096]{1,0:T(8,128)(2,1)S(1)}, bf16[192,4096]{1,0:T(8,128)(2,1)}, u32[]{:S(2)}) copy-start(bf16[192,4096]{1,0:T(8,128)(2,1)} %get-tuple-element.680) | copy-start | bytes 4718596 | tf_op jit(solution)/shard_map/while
  72.0 2.0 copy-start.4
  82.4 133.5 %all-to-all-start = ((bf16[2,16,4096]{2,1,0:T(8,128)(2,1)}), bf16[2,16,4096]{2,1,0:T(8,128)(2,1)}, u32[]{:S(2)}, u32[]{:S(2)}) async-start(bf16[2,16,4096]{2,1,0:T(8,128)(2,1)} %all_to_all.28), calls=%async_computation | async-start | bytes 524288 | tf_op jit(solution)/shard_map/all_to_all | solution.py:190
  159.2 2.4 %copy-start.2 = (bf16[192,4,8,128]{3,0,2,1:T(8,128)(2,1)S(1)}, bf16[192,4,8,128]{3,0,2,1:T(8,128)(2,1)}, u32[]{:S(2)}) copy-start(bf16[192,4,8,128]{3,0,2,1:T(8,128)(2,1)} %get-tuple-element.202) | copy-start | bytes 4718596 | tf_op jit(solution)/shard_map/while/body/eval_jaxpr/cond
  165.2 6.5 %copy-start = (f32[4,768,192,8]{1,2,3,0:T(8,128)}, f32[4,768,192,8]{1,2,3,0:T(8,128)S(1)}, u32[]{:S(2)}) copy-start(f32[4,768,192,8]{1,2,3,0:T(8,128)S(1)} %get-tuple-element.457) | copy-start | bytes 56623108 | tf_op jit(solution)/shard_map/while/body/eval_jaxpr/cond
  190.4 2.4 %copy-start.2 = (bf16[192,4,8,128]{3,0,2,1:T(8,128)(2,1)S(1)}, bf16[192,4,8,128]{3,0,2,1:T(8,128)(2,1)}, u32[]{:S(2)}) copy-start(bf16[192,4,8,128]{3,0,2,1:T(8,128)(2,1)} %get-tuple-element.202) | copy-start | bytes 4718596 | tf_op jit(solution)/shard_map/while/body/eval_jaxpr/cond
  196.3 6.5 %copy-start = (f32[4,768,192,8]{1,2,3,0:T(8,128)}, f32[4,768,192,8]{1,2,3,0:T(8,128)S(1)}, u32[]{:S(2)}) copy-start(f32[4,768,192,8]{1,2,3,0:T(8,128)S(1)} %get-tuple-element.457) | copy-start | bytes 56623108 | tf_op jit(solution)/shard_map/while/body/eval_jaxpr/cond
  215.9 14.7 %all-to-all-start.1 = ((bf16[2,96,4096]{2,1,0:T(8,128)(2,1)}), bf16[2,96,4096]{2,1,0:T(8,128)(2,1)S(1)}, u32[]{:S(2)}, u32[]{:S(2)}) async-start(bf16[2,96,4096]{2,1,0:T(8,128)(2,1)} %all_to_all.32), calls=%async_computation.1 | async-start | bytes 3145728 | tf_op jit(solution)/shard_map/all_to_all | solution.py:191
Sparse Core Ops, SparseCore 0:
  10.7 40.3 all-gather.3
  53.4 44.4 all-gather.5
  100.1 43.8 all-gather.7
